TPU v7x, 32 devices: a whole 2x2x4 slice. The times are simulated.
32 devices in a mesh: gx: 4 (over y, x), gy: 8 (over z, core).
Axes of the slice: x: 2, y: 2, z: 4, core: 2. Of those that a mesh axis runs over, the one named last changes fastest.
Arguments:
- tokens: bfloat16 [4096, 8192], P('gy', 'gx'), may hold values from -6 to 6
- pair_ids: int32 [8], replicated, may hold values from 0 to 7, each once
- query_weight: bfloat16 [8192, 8192], P('gy', 'gx'), may hold values from -0.0625 to 0.0625
- key_matrix: bfloat16 [8192, 1024], P('gy', 'gx'), may hold values from -0.0625 to 0.0625
- value_matrix: bfloat16 [8192, 1024], P('gy', 'gx'), may hold values from -0.0625 to 0.0625
- query_bias: bfloat16 [8192], P('gx'), may hold values from -13 to 13
- key_bias: bfloat16 [1024], P('gx'), may hold values from -8 to 8
- value_offset_bias: bfloat16 [1024], P('gx'), may hold values from -3 to 3
Outputs:
- attn_out: bfloat16 [4096, 8192], P('gy', 'gx')
Inputs may be any that keep to these rules, and one draw needn't show every extreme that they name: `pair_ids`: each number from 0 to 7 appears once.
All inputs are finite; a program needn't handle non-finite values.
Results may differ from a plain program's by a relative error of at most 0.0055.
The roundings to bfloat16 on the way count: a program that leaves them out, or rounds other values in their place, can miss the bound.
Values may be sent and summed in bfloat16 or wider, within the bound.
A program may use at most 128 MiB of HBM per device.

v0:
```python
import math
import jax
import jax.numpy as jnp
from jax import lax
from jax.sharding import PartitionSpec as P

HEAD_SIZE = 128
rope_theta = 1000000.0
neg_large = -1e30


def table_lookup(entries, wanted):
    slot_ids = lax.iota(jnp.int32, entries.shape[0])
    return jnp.sum(jnp.where(wanted[:, None] == slot_ids[None, :], entries[None, :], 0), axis=1)


def layout_positions(pair_ids, total_row_count, tok_dev):
    half_len = tok_dev // 2
    row_ids = lax.iota(jnp.int32, total_row_count)
    within = row_ids % tok_dev
    owners = table_lookup(pair_ids, row_ids // tok_dev)
    mirrored = 2 * pair_ids.shape[0] - 1 - owners
    return jnp.where(
        within < half_len, owners * half_len + within, mirrored * half_len + within - half_len
    )


def apply_rotary(values, token_positions):
    half_size = values.shape[-1] // 2
    frequency = jnp.exp(
        lax.iota(jnp.float32, half_size) * (-2.0 * math.log(rope_theta) / values.shape[-1])
    )
    angles = token_positions.astype(jnp.float32)[:, None] * frequency[None, :]
    cos_part = jnp.cos(angles)[:, None, :]
    sin_part = jnp.sin(angles)[:, None, :]
    lower_half = values[..., :half_size]
    upper_half = values[..., half_size:]
    return jnp.concatenate(
        [
            lower_half * cos_part - upper_half * sin_part,
            upper_half * cos_part + lower_half * sin_part,
        ],
        axis=-1,
    )


def absorb(running, query_block, key_block, value_block, visible):
    row_peak, totals, outputs = running
    scale = 1.0 / math.sqrt(query_block.shape[-1])
    scores = (
        jnp.einsum("hqd,khd->hqk", query_block, key_block, preferred_element_type=jnp.float32)
        * scale
    )
    if visible is not None:
        scores = jnp.where(visible[None], scores, neg_large)
    new_peak = jnp.maximum(row_peak, jnp.max(scores, axis=-1))
    weights = jnp.exp(scores - new_peak[..., None])
    if visible is not None:
        weights = jnp.where(visible[None], weights, 0.0)
    rescale = jnp.exp(row_peak - new_peak)
    totals = totals * rescale + jnp.sum(weights, axis=-1)
    outputs = outputs * rescale[..., None] + jnp.einsum(
        "hqk,khd->hqd",
        weights.astype(jnp.bfloat16),
        value_block,
        preferred_element_type=jnp.float32,
    )
    return (new_peak, totals, outputs)


def on_device(
    tokens,
    pair_ids,
    query_weight,
    key_matrix,
    value_matrix,
    query_bias,
    key_bias,
    value_offset_bias,
):
    tok_dev = tokens.shape[0]
    half_len = tok_dev // 2
    whole_rows = tok_dev * lax.axis_size("gy")
    kv_local = key_matrix.shape[1] // HEAD_SIZE
    q_local = query_weight.shape[1] // HEAD_SIZE
    query_group_width = q_local // kv_local
    gathered = lax.all_gather(tokens, "gx", axis=1, tiled=True)
    stacked = jnp.concatenate([query_weight, key_matrix, value_matrix], axis=1)
    projected = jnp.dot(
        gathered,
        lax.all_gather(stacked, "gy", axis=0, tiled=True),
        preferred_element_type=jnp.float32,
    )
    all_positions = layout_positions(pair_ids, whole_rows, tok_dev)
    own_index = lax.axis_index("gy")
    own_positions = lax.dynamic_slice_in_dim(all_positions, own_index * tok_dev, tok_dev, 0)
    own_pair = table_lookup(pair_ids, jnp.reshape(own_index, (1,)))[0]
    q_cols = q_local * HEAD_SIZE
    kv_cols = kv_local * HEAD_SIZE
    queries = projected[:, :q_cols] + query_bias.astype(jnp.float32)
    queries = apply_rotary(queries.reshape(tok_dev, q_local, HEAD_SIZE), own_positions).astype(
        jnp.bfloat16
    )
    projected_key_rows = projected[:, q_cols : q_cols + kv_cols] + key_bias.astype(jnp.float32)
    projected_key_rows = (
        apply_rotary(projected_key_rows.reshape(tok_dev, kv_local, HEAD_SIZE), own_positions)
        .astype(jnp.bfloat16)
        .reshape(tok_dev, kv_cols)
    )
    projected_value_rows = (
        projected[:, q_cols + kv_cols :] + value_offset_bias.astype(jnp.float32)
    ).astype(jnp.bfloat16)
    query_rows = (
        queries.reshape(tok_dev, kv_local, query_group_width, HEAD_SIZE)
        .transpose(1, 0, 2, 3)
        .reshape(kv_local, tok_dev * query_group_width, HEAD_SIZE)
    )
    row_positions = jnp.repeat(own_positions, query_group_width)
    row_total = tok_dev * query_group_width
    initial = (
        jnp.full((kv_local, row_total), neg_large, jnp.float32),
        jnp.zeros((kv_local, row_total), jnp.float32),
        jnp.zeros((kv_local, row_total, HEAD_SIZE), jnp.float32),
    )

    def paired(running, key_shard, value_shard, earlier):
        cut_rows = half_len * query_group_width
        former = tuple((member[:, :cut_rows] for member in running))
        latter = tuple((member[:, cut_rows:] for member in running))
        query_former = query_rows[:, :cut_rows]
        query_latter = query_rows[:, cut_rows:]
        latter = absorb(latter, query_latter, key_shard[:half_len], value_shard[:half_len], None)
        picked_state = tuple(
            (jnp.where(earlier, left, right) for left, right in zip(former, latter))
        )
        query_pick = jnp.where(earlier, query_former, query_latter)
        key_pick = jnp.where(earlier, key_shard[:half_len], key_shard[half_len:])
        value_pick = jnp.where(earlier, value_shard[:half_len], value_shard[half_len:])
        updated = absorb(picked_state, query_pick, key_pick, value_pick, None)
        former = tuple((jnp.where(earlier, fresh, kept) for fresh, kept in zip(updated, former)))
        latter = tuple((jnp.where(earlier, kept, fresh) for fresh, kept in zip(updated, latter)))
        return tuple(
            (jnp.concatenate([left, right], axis=1) for left, right in zip(former, latter))
        )

    key_piece = lax.all_gather(projected_key_rows, "gy", axis=0, tiled=True)
    value_piece = lax.all_gather(projected_value_rows, "gy", axis=0, tiled=True)
    total_row_count = key_piece.shape[0]

    def one_shard(shard_index, carried):
        begin = shard_index * tok_dev
        key_shard = lax.dynamic_slice_in_dim(key_piece, begin, tok_dev, 0).reshape(
            tok_dev, kv_local, HEAD_SIZE
        )
        value_shard = lax.dynamic_slice_in_dim(value_piece, begin, tok_dev, 0).reshape(
            tok_dev, kv_local, HEAD_SIZE
        )
        source = jnp.reshape(begin // tok_dev, (1,))
        their_pair = table_lookup(pair_ids, source)[0]

        def itself(state_in):
            key_positions = lax.dynamic_slice_in_dim(all_positions, begin, tok_dev, 0)
            visible = key_positions[None, :] <= row_positions[:, None]
            return absorb(state_in, query_rows, key_shard, value_shard, visible)

        def elsewhere(state_in):
            return paired(state_in, key_shard, value_shard, their_pair < own_pair)

        return lax.cond(their_pair == own_pair, itself, elsewhere, carried)

    row_peak, totals, outputs = lax.fori_loop(0, total_row_count // tok_dev, one_shard, initial)
    normalized = (outputs / totals[..., None]).astype(jnp.bfloat16)
    return (
        normalized.reshape(kv_local, tok_dev, query_group_width, HEAD_SIZE)
        .transpose(1, 0, 2, 3)
        .reshape(tok_dev, q_cols)
    )


def solution(mesh):
    in_specs = (
        P("gy", "gx"),
        P(),
        P("gy", "gx"),
        P("gy", "gx"),
        P("gy", "gx"),
        P("gx"),
        P("gx"),
        P("gx"),
    )
    out_specs = P("gy", "gx")
    return jax.shard_map(
        on_device, mesh=mesh, in_specs=in_specs, out_specs=out_specs, check_vma=False
    )
```

profile of v0, /device:TPU:0, one launch (start us, length us, event | category | flops | bytes accessed | tf_op | source)
XLA Modules:
  0.0 768.3 jit_solution(7641844237663635094)
XLA Ops:
  7.3 6.9 pad_maximum_fusion.3
  15.7 83.8 %all-gather.7.cloned.1.call-done = bf16[512,8192]{1,0:T(8,128)(2,1)} async-done(((bf16[512,2048]{1,0:T(8,128)(2,1)}), bf16[512,8192]{1,0:T(8,128)(2,1)}) %all-gather.7.cloned.1.call-update) | async-done | bytes 8388624 | tf_op jit(solution)/shard_map/all_gather | solution.py:87
  99.4 360.5 %all-gather.5.cloned.1.call-done = bf16[8192,2560]{1,0:T(8,128)(2,1)} async-done(((bf16[1024,2560]{1,0:T(8,128)(2,1)}), bf16[8192,2560]{1,0:T(8,128)(2,1)}) %all-gather.5.cloned.1.call-update) | async-done | bytes 41943056 | tf_op jit(solution)/shard_map/all_gather | solution.py:91
  459.9 30.0 %convolution_bitcast_fusion = f32[512,2560]{0,1:T(8,128)} fusion(bf16[8192,2560]{1,0:T(8,128)(2,1)} %all-gather.5.cloned.1.call-done, bf16[512,8192]{1,0:T(8,128)(2,1)} %all-gather.7.cloned.1.call-done), kind=kOutput, calls=%fused_computation.67 | convolution fusion | flops 21474836480 | bytes 55574528 | tf_op jit(solution)/shard_map/dot_general | solution.py:89
  503.4 4.1 maximum_bitcast_fusion
  507.5 13.1 %all-gather.9.cloned.1.call-done = bf16[4096,256]{0,1:T(8,128)(2,1)} async-done(((bf16[512,256]{0,1:T(8,128)(2,1)}), bf16[4096,256]{0,1:T(8,128)(2,1)}) %all-gather.9.cloned.1.call-update) | async-done | bytes 2097168 | tf_op jit(solution)/shard_map/all_gather | solution.py:146
  520.6 30.0 %all-gather.11.cloned.1.call-done = bf16[4096,256]{0,1:T(8,128)(2,1)} async-done(((bf16[512,256]{0,1:T(8,128)(2,1)}), bf16[4096,256]{0,1:T(8,128)(2,1)}) %all-gather.11.cloned.1.call-update) | async-done | bytes 2097168 | tf_op jit(solution)/shard_map/all_gather | solution.py:147
  553.5 203.1 %while.20 = (s32[]{:T(128)}, f32[2,4096]{1,0:T(2,128)S(1)}, f32[2,4096]{1,0:T(2,128)}, f32[2,4096,128]{2,1,0:T(8,128)}, s32[8]{0:T(128)S(1)}, /*index=5*/s32[]{:...) while((s32[]{:T(128)}, f32[2,4096]{1,0:T(2,128)S(1)}, ...), condition=%wide.region_12.13_spmd.clone, body=%wide.region_2.12_spmd.clone.sunk | while | flops 2206220288 | bytes 138748624 | solution.py:171
  556.6 28.6 %conditional.3 = (f32[2,4096]{1,0:T(2,128)}, f32[2,4096]{1,0:T(2,128)}, f32[2,4096,128]{2,1,0:T(8,128)}) conditional(s32[]{:T(128)} %convert_element_type.69, (s32[]{:T(128)}, s32[]{:T(128)}, f32[2,4096]{1,0:T(2,128)S(1)}, bf16[2,4096,128]{2,1,0:T(8,128)(2,1)}, bf16[512,2,128]{0,2,1:T(8,128)(2,1)S(1)}, /*index=5*/f32[2,4096]{1,0:T(2,128)}, ...), branch_computations={%region_4.8_spmd, %region_9.11_spmd} | conditional | flops 2206220288 | bytes 137633952 | solution.py:169
  558.3 5.8 fusion.28
  566.1 5.3 fusion.30
  572.9 12.3 %fusion.34 = f32[2,4096,128]{2,1,0:T(8,128)} fusion(bf16[512,2,128]{0,2,1:T(8,128)(2,1)S(1)} %get-tuple-element.414, f32[2,4096,512]{1,2,0:T(8,128)} %copy-done.3, f32[2,4096]{1,0:T(2,128)} %max.8, pred[4096,512]{0,1:T(8,128)(4,1)S(1)} %broadcast_compare_fusion, f32[2,4096,128]{2,1,0:T(8,128)} %get-tuple-element.321, f32[2,4096]{1,0:T(2,128)S(1)} %get-tuple-element.446), kind=kOutput, calls=%fused_computation.55 | convolution fusion | flops 1096810496 | bytes 27590656 | tf_op jit(solution)/shard_map/while/body/eval_jaxpr/cond/branch_1_fun/hqk,khd->hqd/dot_general | solution.py:62
  589.0 20.6 %conditional.3 = (f32[2,4096]{1,0:T(2,128)}, f32[2,4096]{1,0:T(2,128)}, f32[2,4096,128]{2,1,0:T(8,128)}) conditional(s32[]{:T(128)} %convert_element_type.69, (s32[]{:T(128)}, s32[]{:T(128)}, f32[2,4096]{1,0:T(2,128)S(1)}, bf16[2,4096,128]{2,1,0:T(8,128)(2,1)}, bf16[512,2,128]{0,2,1:T(8,128)(2,1)S(1)}, /*index=5*/f32[2,4096]{1,0:T(2,128)}, ...), branch_computations={%region_4.8_spmd, %region_9.11_spmd} | conditional | flops 2206220288 | bytes 137633952 | solution.py:169
  598.4 4.4 convolution_add_fusion.1
  613.4 20.6 %conditional.3 = (f32[2,4096]{1,0:T(2,128)}, f32[2,4096]{1,0:T(2,128)}, f32[2,4096,128]{2,1,0:T(8,128)}) conditional(s32[]{:T(128)} %convert_element_type.69, (s32[]{:T(128)}, s32[]{:T(128)}, f32[2,4096]{1,0:T(2,128)S(1)}, bf16[2,4096,128]{2,1,0:T(8,128)(2,1)}, bf16[512,2,128]{0,2,1:T(8,128)(2,1)S(1)}, /*index=5*/f32[2,4096]{1,0:T(2,128)}, ...), branch_computations={%region_4.8_spmd, %region_9.11_spmd} | conditional | flops 2206220288 | bytes 137633952 | solution.py:169
  617.1 2.8 multiply_reduce_fusion.1
  622.8 4.4 convolution_add_fusion.1
  637.8 20.6 %conditional.3 = (f32[2,4096]{1,0:T(2,128)}, f32[2,4096]{1,0:T(2,128)}, f32[2,4096,128]{2,1,0:T(8,128)}) conditional(s32[]{:T(128)} %convert_element_type.69, (s32[]{:T(128)}, s32[]{:T(128)}, f32[2,4096]{1,0:T(2,128)S(1)}, bf16[2,4096,128]{2,1,0:T(8,128)(2,1)}, bf16[512,2,128]{0,2,1:T(8,128)(2,1)S(1)}, /*index=5*/f32[2,4096]{1,0:T(2,128)}, ...), branch_computations={%region_4.8_spmd, %region_9.11_spmd} | conditional | flops 2206220288 | bytes 137633952 | solution.py:169
  641.5 2.8 multiply_reduce_fusion.1
  647.2 4.4 convolution_add_fusion.1
  662.2 20.6 %conditional.3 = (f32[2,4096]{1,0:T(2,128)}, f32[2,4096]{1,0:T(2,128)}, f32[2,4096,128]{2,1,0:T(8,128)}) conditional(s32[]{:T(128)} %convert_element_type.69, (s32[]{:T(128)}, s32[]{:T(128)}, f32[2,4096]{1,0:T(2,128)S(1)}, bf16[2,4096,128]{2,1,0:T(8,128)(2,1)}, bf16[512,2,128]{0,2,1:T(8,128)(2,1)S(1)}, /*index=5*/f32[2,4096]{1,0:T(2,128)}, ...), branch_computations={%region_4.8_spmd, %region_9.11_spmd} | conditional | flops 2206220288 | bytes 137633952 | solution.py:169
  665.9 2.8 multiply_reduce_fusion.1
  671.6 4.4 convolution_add_fusion.1
  686.6 20.6 %conditional.3 = (f32[2,4096]{1,0:T(2,128)}, f32[2,4096]{1,0:T(2,128)}, f32[2,4096,128]{2,1,0:T(8,128)}) conditional(s32[]{:T(128)} %convert_element_type.69, (s32[]{:T(128)}, s32[]{:T(128)}, f32[2,4096]{1,0:T(2,128)S(1)}, bf16[2,4096,128]{2,1,0:T(8,128)(2,1)}, bf16[512,2,128]{0,2,1:T(8,128)(2,1)S(1)}, /*index=5*/f32[2,4096]{1,0:T(2,128)}, ...), branch_computations={%region_4.8_spmd, %region_9.11_spmd} | conditional | flops 2206220288 | bytes 137633952 | solution.py:169
  690.3 2.8 multiply_reduce_fusion.1
  696.0 4.4 convolution_add_fusion.1
  710.9 20.6 %conditional.3 = (f32[2,4096]{1,0:T(2,128)}, f32[2,4096]{1,0:T(2,128)}, f32[2,4096,128]{2,1,0:T(8,128)}) conditional(s32[]{:T(128)} %convert_element_type.69, (s32[]{:T(128)}, s32[]{:T(128)}, f32[2,4096]{1,0:T(2,128)S(1)}, bf16[2,4096,128]{2,1,0:T(8,128)(2,1)}, bf16[512,2,128]{0,2,1:T(8,128)(2,1)S(1)}, /*index=5*/f32[2,4096]{1,0:T(2,128)}, ...), branch_computations={%region_4.8_spmd, %region_9.11_spmd} | conditional | flops 2206220288 | bytes 137633952 | solution.py:169
  720.4 4.4 convolution_add_fusion.1
  735.3 20.6 %conditional.3 = (f32[2,4096]{1,0:T(2,128)}, f32[2,4096]{1,0:T(2,128)}, f32[2,4096,128]{2,1,0:T(8,128)}) conditional(s32[]{:T(128)} %convert_element_type.69, (s32[]{:T(128)}, s32[]{:T(128)}, f32[2,4096]{1,0:T(2,128)S(1)}, bf16[2,4096,128]{2,1,0:T(8,128)(2,1)}, bf16[512,2,128]{0,2,1:T(8,128)(2,1)S(1)}, /*index=5*/f32[2,4096]{1,0:T(2,128)}, ...), branch_computations={%region_4.8_spmd, %region_9.11_spmd} | conditional | flops 2206220288 | bytes 137633952 | solution.py:169
  739.1 2.8 multiply_reduce_fusion.1
  744.8 4.4 convolution_add_fusion.1
  756.7 2.9 fusion.41
  (209 shorter events, 136.1 us)
Async XLA Ops:
  6.5 92.9 %all-gather.7.cloned.1.call-start = ((), (), s32[]{:S(2)}) async-start(), calls=%async_computation.1 | async-start | bytes 10485760 | tf_op jit(solution)/shard_map/all_gather | solution.py:87
  7.3 452.7 %all-gather.5.cloned.1.call-start = ((), (), s32[]{:S(2)}) async-start(), calls=%async_computation | async-start | bytes 47185920 | tf_op jit(solution)/shard_map/all_gather | solution.py:91
  14.2 506.4 %all-gather.9.cloned.1.call-start = ((), (), s32[]{:S(2)}) async-start(), calls=%async_computation.2 | async-start | bytes 2359296 | tf_op jit(solution)/shard_map/all_gather | solution.py:146
  15.6 477.7 %copy-start.7 = (bf16[2048]{0:T(1024)(128)(2,1)S(1)}, bf16[2048]{0:T(1024)(128)(2,1)}, u32[]{:S(2)}) copy-start(bf16[2048]{0:T(1024)(128)(2,1)} %param.17) | copy-start | bytes 12292
  492.8 57.9 %all-gather.11.cloned.1.call-start = ((), (), s32[]{:S(2)}) async-start(), calls=%async_computation.3 | async-start | bytes 2359296 | tf_op jit(solution)/shard_map/all_gather | solution.py:147
  564.2 7.2 copy-start.3
  566.1 5.3 copy-start.6
  592.7 4.3 copy-start
  595.5 2.0 copy-start.2
  598.4 4.4 copy-start.1
  598.4 5.3 copy-start.4
  617.1 4.3 copy-start
  619.9 2.0 copy-start.2
  622.8 4.4 copy-start.1
  622.8 5.3 copy-start.4
  641.5 4.3 copy-start
  644.3 2.0 copy-start.2
  647.2 4.4 copy-start.1
  647.2 5.3 copy-start.4
  665.9 4.3 copy-start
  668.6 2.0 copy-start.2
  671.6 4.4 copy-start.1
  671.6 5.3 copy-start.4
  690.3 4.3 copy-start
  696.0 4.4 copy-start.1
  696.0 5.3 copy-start.4
  714.7 4.3 copy-start
  720.4 4.4 copy-start.1
  720.4 5.3 copy-start.4
  739.0 4.3 copy-start
  744.8 4.4 copy-start.1
  744.8 5.3 copy-start.4
  (7 other events, 9.6 us)
Sparse Core Ops, SparseCore 0:
  9.2 90.1 all-gather.6
  101.1 358.8 all-gather.4
  492.9 27.7 all-gather.8
  522.1 28.5 all-gather.10
where the time goes:
time: 771 us; the launch traced here: 768 us
  waiting for transfers between devices  489 us (63%)
  matrix products  126 us (16%)
  other arithmetic  83.3 us (11%)
  local copies, waits for them, and re-layouts  37.8 us (5%)
  loops' own time  19.6 us (3%)
  between operations  13.2 us (2%)
    all_gather x1, waiting for transfers between devices, on_device(): lax.all_gather(stacked, 'gy', axis=0, tiled=True)  361 us
    all_gather x1, waiting for transfers between devices, on_device(): gathered = lax.all_gather(tokens, 'gx', axis=1, tiled=True)  83.8 us
    dot_general x15, matrix products, absorb(): jnp.einsum('hqk,khd->hqd', weights.astype(jnp.bfloat16), value_block, pre...  54.5 us
    dot_general x15, matrix products, absorb(): jnp.einsum('hqd,khd->hqk', query_block, key_block, preferred_element_type...  41.1 us
    all_gather x1, waiting for transfers between devices, on_device(): value_piece = lax.all_gather(projected_value_rows, 'gy', axis=0, tiled=True)  30 us
    dot_general x1, matrix products, on_device(): jnp.dot(gathered, lax.all_gather(stacked, 'gy', axis=0, tiled=True), pref...  30 us
    concatenate x21, other arithmetic, paired(): jnp.concatenate([left, right], axis=1)  24.3 us
    reduce_sum x8, other arithmetic, absorb(): totals = totals * rescale + jnp.sum(weights, axis=-1)  15.5 us
  transfers between devices with their start and end apart: 4, of which 4 were waited for; matrix products, arithmetic and copies ran while one was open for 3% of the time, Pallas kernels for 0%

commit v1 on v0

--- a/solution.py
+++ b/solution.py
@@ -88,7 +88,9 @@
     stacked = jnp.concatenate([query_weight, key_matrix, value_matrix], axis=1)
     projected = jnp.dot(
         gathered,
-        lax.all_gather(stacked, "gy", axis=0, tiled=True),
+        jnp.concatenate(
+            lax.all_to_all(jnp.stack([stacked] * lax.axis_size("gy")), "gy", 0, 0), axis=0
+        ),
         preferred_element_type=jnp.float32,
     )
     all_positions = layout_positions(pair_ids, whole_rows, tok_dev)

time: 771 us -> 1250 us (1.62)
  waiting for transfers between devices: 489 us -> 947 us
  local copies, waits for them, and re-layouts: 37.8 us -> 51 us
    all_to_all x0 -> x1, waiting for transfers between devices: none -> 811 us  [on_device(): lax.all_to_all(jnp.stack([stacked] * lax.axis_size('gy')), 'gy', 0, 0)]
    all_gather x1 -> x0, waiting for transfers between devices: 361 us -> none  [on_device(): lax.all_gather(stacked, 'gy', axis=0, tiled=True)]
    another operation x14 -> x15, local copies, waits for them, and re-layouts: 2.36 us -> 16.2 us  [the longest x1 13.8 us: on_device(): jnp.stack([stacked] * lax.axis_size('gy'))]
  transfers between devices with their start and end apart: 4 -> 4, of which waited for: 4 -> 4; matrix products, arithmetic and copies ran while one was open for 3% -> 1% of each run, Pallas kernels for 0% -> 0%
where the time goes in v1:
time: 1250 us
  waiting for transfers between devices  947 us (76%)
  matrix products  126 us (10%)
  other arithmetic  80.3 us (6%)
  local copies, waits for them, and re-layouts  51 us (4%)
  loops' own time  19.6 us (2%)
  between operations  13.3 us (1%)
    all_to_all x1, waiting for transfers between devices, on_device(): lax.all_to_all(jnp.stack([stacked] * lax.axis_size('gy')), 'gy', 0, 0)  811 us
    all_gather x1, waiting for transfers between devices, on_device(): gathered = lax.all_gather(tokens, 'gx', axis=1, tiled=True)  91.4 us
    dot_general x15, matrix products, absorb(): jnp.einsum('hqk,khd->hqd', weights.astype(jnp.bfloat16), value_block, pre...  54.5 us
    dot_general x15, matrix products, absorb(): jnp.einsum('hqd,khd->hqk', query_block, key_block, preferred_element_type...  41.1 us
    all_gather x1, waiting for transfers between devices, on_device(): value_piece = lax.all_gather(projected_value_rows, 'gy', axis=0, tiled=True)  30.2 us
    dot_general x1, matrix products, on_device(): jnp.dot(gathered, jnp.concatenate(lax.all_to_all(jnp.stack([stacked] * la...  30 us
  transfers between devices with their start and end apart: 4, of which 4 were waited for; matrix products, arithmetic and copies ran while one was open for 1% of the time, Pallas kernels for 0%

profile of v1, /device:TPU:0, one launch (start us, length us, event | category | flops | bytes accessed | tf_op | source)
XLA Modules:
  0.0 1245.5 jit_solution(17334891910721846979)
XLA Ops:
  6.5 4.5 pad_maximum_fusion.3
  11.0 13.8 %stack.2 = bf16[8,1024,2560]{2,1,0:T(8,128)(2,1)} broadcast(bf16[1024,2560]{1,0:T(8,128)(2,1)S(1)} %pad_maximum_fusion.3), dimensions={1,2} | broadcast | bytes 47185920 | tf_op jit(solution)/shard_map/stack | solution.py:92
  24.8 7.9 all-to-all-start
  34.4 91.4 %all-gather.4.cloned.1.call-done = bf16[512,8192]{1,0:T(8,128)(2,1)} async-done(((bf16[512,2048]{1,0:T(8,128)(2,1)}), bf16[512,8192]{1,0:T(8,128)(2,1)}) %all-gather.4.cloned.1.call-update) | async-done | bytes 8388624 | tf_op jit(solution)/shard_map/all_gather | solution.py:87
  125.8 810.8 %all-to-all-done = bf16[8,1024,2560]{2,1,0:T(8,128)(2,1)} async-done(((bf16[8,1024,2560]{2,1,0:T(8,128)(2,1)}), bf16[8,1024,2560]{2,1,0:T(8,128)(2,1)}, u32[]{:S(2)}, u32[]{:S(2)}) %all-to-all-start) | async-done | bytes 41943072 | tf_op jit(solution)/shard_map/all_to_all | solution.py:92
  936.7 30.0 %convolution_bitcast_fusion = f32[512,2560]{0,1:T(8,128)} fusion(bf16[8192,2560]{1,0:T(8,128)(2,1)} %bitcast, bf16[512,8192]{1,0:T(8,128)(2,1)} %all-gather.4.cloned.1.call-done), kind=kOutput, calls=%fused_computation.67 | convolution fusion | flops 21474836480 | bytes 55574528 | tf_op jit(solution)/shard_map/dot_general | solution.py:89
  980.4 4.1 maximum_bitcast_fusion
  984.5 13.8 %all-gather.6.cloned.1.call-done = bf16[4096,256]{0,1:T(8,128)(2,1)} async-done(((bf16[512,256]{0,1:T(8,128)(2,1)}), bf16[4096,256]{0,1:T(8,128)(2,1)}) %all-gather.6.cloned.1.call-update) | async-done | bytes 2097168 | tf_op jit(solution)/shard_map/all_gather | solution.py:148
  998.3 30.2 %all-gather.8.cloned.1.call-done = bf16[4096,256]{0,1:T(8,128)(2,1)} async-done(((bf16[512,256]{0,1:T(8,128)(2,1)}), bf16[4096,256]{0,1:T(8,128)(2,1)}) %all-gather.8.cloned.1.call-update) | async-done | bytes 2097168 | tf_op jit(solution)/shard_map/all_gather | solution.py:149
  1031.4 202.5 %while.20 = (s32[]{:T(128)}, f32[2,4096]{1,0:T(2,128)S(1)}, f32[2,4096]{1,0:T(2,128)}, f32[2,4096,128]{2,1,0:T(8,128)}, s32[8]{0:T(128)S(1)}, /*index=5*/s32[]{:...) while((s32[]{:T(128)}, f32[2,4096]{1,0:T(2,128)S(1)}, ...), condition=%wide.region_12.13_spmd.clone, body=%wide.region_2.12_spmd.clone.sunk | while | flops 2206220288 | bytes 138748624 | solution.py:173
  1034.3 28.6 %conditional.3 = (f32[2,4096]{1,0:T(2,128)}, f32[2,4096]{1,0:T(2,128)}, f32[2,4096,128]{2,1,0:T(8,128)}) conditional(s32[]{:T(128)} %convert_element_type.69, (s32[]{:T(128)}, s32[]{:T(128)}, f32[2,4096]{1,0:T(2,128)S(1)}, bf16[2,4096,128]{2,1,0:T(8,128)(2,1)}, bf16[512,2,128]{0,2,1:T(8,128)(2,1)S(1)}, /*index=5*/f32[2,4096]{1,0:T(2,128)}, ...), branch_computations={%region_4.8_spmd, %region_9.11_spmd} | conditional | flops 2206220288 | bytes 137633952 | solution.py:171
  1036.0 5.8 fusion.28
  1043.8 5.3 fusion.30
  1050.6 12.3 fusion.34
  1066.7 20.6 %conditional.3 = (f32[2,4096]{1,0:T(2,128)}, f32[2,4096]{1,0:T(2,128)}, f32[2,4096,128]{2,1,0:T(8,128)}) conditional(s32[]{:T(128)} %convert_element_type.69, (s32[]{:T(128)}, s32[]{:T(128)}, f32[2,4096]{1,0:T(2,128)S(1)}, bf16[2,4096,128]{2,1,0:T(8,128)(2,1)}, bf16[512,2,128]{0,2,1:T(8,128)(2,1)S(1)}, /*index=5*/f32[2,4096]{1,0:T(2,128)}, ...), branch_computations={%region_4.8_spmd, %region_9.11_spmd} | conditional | flops 2206220288 | bytes 137633952 | solution.py:171
  1070.4 2.8 multiply_reduce_fusion.1
  1076.1 4.4 convolution_add_fusion.1
  1091.0 20.6 %conditional.3 = (f32[2,4096]{1,0:T(2,128)}, f32[2,4096]{1,0:T(2,128)}, f32[2,4096,128]{2,1,0:T(8,128)}) conditional(s32[]{:T(128)} %convert_element_type.69, (s32[]{:T(128)}, s32[]{:T(128)}, f32[2,4096]{1,0:T(2,128)S(1)}, bf16[2,4096,128]{2,1,0:T(8,128)(2,1)}, bf16[512,2,128]{0,2,1:T(8,128)(2,1)S(1)}, /*index=5*/f32[2,4096]{1,0:T(2,128)}, ...), branch_computations={%region_4.8_spmd, %region_9.11_spmd} | conditional | flops 2206220288 | bytes 137633952 | solution.py:171
  1094.7 2.8 multiply_reduce_fusion.1
  1100.4 4.4 convolution_add_fusion.1
  1115.3 20.6 %conditional.3 = (f32[2,4096]{1,0:T(2,128)}, f32[2,4096]{1,0:T(2,128)}, f32[2,4096,128]{2,1,0:T(8,128)}) conditional(s32[]{:T(128)} %convert_element_type.69, (s32[]{:T(128)}, s32[]{:T(128)}, f32[2,4096]{1,0:T(2,128)S(1)}, bf16[2,4096,128]{2,1,0:T(8,128)(2,1)}, bf16[512,2,128]{0,2,1:T(8,128)(2,1)S(1)}, /*index=5*/f32[2,4096]{1,0:T(2,128)}, ...), branch_computations={%region_4.8_spmd, %region_9.11_spmd} | conditional | flops 2206220288 | bytes 137633952 | solution.py:171
  1119.0 2.8 multiply_reduce_fusion.1
  1124.7 4.4 convolution_add_fusion.1
  1139.6 20.6 %conditional.3 = (f32[2,4096]{1,0:T(2,128)}, f32[2,4096]{1,0:T(2,128)}, f32[2,4096,128]{2,1,0:T(8,128)}) conditional(s32[]{:T(128)} %convert_element_type.69, (s32[]{:T(128)}, s32[]{:T(128)}, f32[2,4096]{1,0:T(2,128)S(1)}, bf16[2,4096,128]{2,1,0:T(8,128)(2,1)}, bf16[512,2,128]{0,2,1:T(8,128)(2,1)S(1)}, /*index=5*/f32[2,4096]{1,0:T(2,128)}, ...), branch_computations={%region_4.8_spmd, %region_9.11_spmd} | conditional | flops 2206220288 | bytes 137633952 | solution.py:171
  1149.0 4.4 convolution_add_fusion.1
  1163.9 20.6 %conditional.3 = (f32[2,4096]{1,0:T(2,128)}, f32[2,4096]{1,0:T(2,128)}, f32[2,4096,128]{2,1,0:T(8,128)}) conditional(s32[]{:T(128)} %convert_element_type.69, (s32[]{:T(128)}, s32[]{:T(128)}, f32[2,4096]{1,0:T(2,128)S(1)}, bf16[2,4096,128]{2,1,0:T(8,128)(2,1)}, bf16[512,2,128]{0,2,1:T(8,128)(2,1)S(1)}, /*index=5*/f32[2,4096]{1,0:T(2,128)}, ...), branch_computations={%region_4.8_spmd, %region_9.11_spmd} | conditional | flops 2206220288 | bytes 137633952 | solution.py:171
  1173.4 4.4 convolution_add_fusion.1
  1188.2 20.6 %conditional.3 = (f32[2,4096]{1,0:T(2,128)}, f32[2,4096]{1,0:T(2,128)}, f32[2,4096,128]{2,1,0:T(8,128)}) conditional(s32[]{:T(128)} %convert_element_type.69, (s32[]{:T(128)}, s32[]{:T(128)}, f32[2,4096]{1,0:T(2,128)S(1)}, bf16[2,4096,128]{2,1,0:T(8,128)(2,1)}, bf16[512,2,128]{0,2,1:T(8,128)(2,1)S(1)}, /*index=5*/f32[2,4096]{1,0:T(2,128)}, ...), branch_computations={%region_4.8_spmd, %region_9.11_spmd} | conditional | flops 2206220288 | bytes 137633952 | solution.py:171
  1197.7 4.4 convolution_add_fusion.1
  1212.5 20.6 %conditional.3 = (f32[2,4096]{1,0:T(2,128)}, f32[2,4096]{1,0:T(2,128)}, f32[2,4096,128]{2,1,0:T(8,128)}) conditional(s32[]{:T(128)} %convert_element_type.69, (s32[]{:T(128)}, s32[]{:T(128)}, f32[2,4096]{1,0:T(2,128)S(1)}, bf16[2,4096,128]{2,1,0:T(8,128)(2,1)}, bf16[512,2,128]{0,2,1:T(8,128)(2,1)S(1)}, /*index=5*/f32[2,4096]{1,0:T(2,128)}, ...), branch_computations={%region_4.8_spmd, %region_9.11_spmd} | conditional | flops 2206220288 | bytes 137633952 | solution.py:171
  1222.0 4.4 convolution_add_fusion.1
  1233.9 2.9 fusion.41
  (209 shorter events, 140.6 us)
Async XLA Ops:
  24.8 8.8 copy-start.9
  24.8 8.8 copy-start.10
  24.8 8.8 copy-start.8
  24.8 911.8 %all-to-all-start = ((bf16[8,1024,2560]{2,1,0:T(8,128)(2,1)}), bf16[8,1024,2560]{2,1,0:T(8,128)(2,1)}, u32[]{:S(2)}, u32[]{:S(2)}) async-start(bf16[8,1024,2560]{2,1,0:T(8,128)(2,1)} %stack.2), calls=%async_computation | async-start | bytes 83886080 | tf_op jit(solution)/shard_map/all_to_all | solution.py:92
  32.8 93.0 %all-gather.4.cloned.1.call-start = ((), (), s32[]{:S(2)}) async-start(), calls=%async_computation.1 | async-start | bytes 10485760 | tf_op jit(solution)/shard_map/all_gather | solution.py:87
  33.5 964.8 %all-gather.6.cloned.1.call-start = ((), (), s32[]{:S(2)}) async-start(), calls=%async_computation.2 | async-start | bytes 2359296 | tf_op jit(solution)/shard_map/all_gather | solution.py:148
  936.6 33.6 %copy-start.7 = (bf16[2048]{0:T(1024)(128)(2,1)S(1)}, bf16[2048]{0:T(1024)(128)(2,1)}, u32[]{:S(2)}) copy-start(bf16[2048]{0:T(1024)(128)(2,1)} %param.17) | copy-start | bytes 12292
  969.5 59.0 %all-gather.8.cloned.1.call-start = ((), (), s32[]{:S(2)}) async-start(), calls=%async_computation.3 | async-start | bytes 2359296 | tf_op jit(solution)/shard_map/all_gather | solution.py:149
  1041.9 7.2 copy-start.3
  1043.8 5.3 copy-start.6
  1070.4 4.3 copy-start
  1073.1 2.0 copy-start.2
  1076.1 4.4 copy-start.1
  1076.1 5.3 copy-start.4
  1094.7 4.3 copy-start
  1100.4 4.4 copy-start.1
  1100.4 5.3 copy-start.4
  1119.0 4.3 copy-start
  1124.7 4.4 copy-start.1
  1124.7 5.3 copy-start.4
  1143.3 4.3 copy-start
  1149.0 4.4 copy-start.1
  1149.0 5.3 copy-start.4
  1167.6 4.3 copy-start
  1173.3 4.4 copy-start.1
  1173.3 5.3 copy-start.4
  1191.9 4.3 copy-start
  1197.6 4.4 copy-start.1
  1197.7 5.3 copy-start.4
  1216.2 4.3 copy-start
  1222.0 4.4 copy-start.1
  1222.0 5.3 copy-start.4
  (7 other events, 13.6 us)
Sparse Core Ops, SparseCore 0:
  35.5 90.3 all-gather.3
  969.7 28.6 all-gather.5
  999.9 28.5 all-gather.7
